TPU v7x, 32 devices: a whole 2x2x4 slice. The times are simulated.
32 devices in a mesh: slab: 8 (over z, x), rhs: 4 (over y, core).
Axes of the slice: x: 2, y: 2, z: 4, core: 2. Of those that a mesh axis runs over, the one named last changes fastest.
Arguments:
- targets: float32 [8, 128, 256], P('rhs', 'slab'), may hold values from -60 to 60
- counts: int32 [128], P('slab'), may hold values from 1 to 256, 20480 in all
- cell_rows: int32 [128, 256], P('slab'), may hold values from 0 to 255
- cell_cols: int32 [128, 256], P('slab'), may hold values from 0 to 127
- fractions: float32 [2, 128, 256], P(None, 'slab'), may hold values from 0 to 1
- spectrum: float32 [2048, 2048], P(None, ('slab', 'rhs')), may hold values from 0.25 to 4, as said below
- noise_var: float32 [1], replicated, may hold values from 0.1 to 1
Outputs:
- solution: float32 [8, 128, 256], P('rhs', 'slab')
- residual: float32 [8, 128, 256], P('rhs', 'slab')
Inputs may be any that keep to these rules, and one draw needn't show every extreme that they name: Each tile has 256 slots; tile t holds points in its first counts[t] slots, and the other slots are empty: their entries are ignored and their outputs are zero. Even in frequency: spectrum[a, b] = spectrum[(2048 - a) % 2048, (2048 - b) % 2048].
All inputs are finite; a program needn't handle non-finite values. No bound on the sum of `counts` on one device may be relied on, other than what follows from the above.
Results may differ from a plain program's by a relative error of at most 0.0002.
Values sent between devices are 32-bit elements; how exact they have to be, the bound alone decides.
A program may use at most 128 MiB of HBM per device.

v0:
```python
import functools
import math

import jax
import jax.numpy as jnp
import numpy as np
from jax import lax
from jax.experimental import pallas as pl
from jax.experimental.pallas import tpu as pltpu
from jax.sharding import PartitionSpec as P

G = 2048
TC = 128
ITERS = 2
RADIX = 8
LONG = G // RADIX
RIM = 8
PARTS = 1
F32 = jnp.float32
BF16 = jnp.bfloat16


def cubic_weights(fraction):
    return (
        ((-0.5 * fraction + 1.0) * fraction - 0.5) * fraction,
        (1.5 * fraction - 2.5) * fraction * fraction + 1.0,
        ((-1.5 * fraction + 2.0) * fraction + 0.5) * fraction,
        (0.5 * fraction - 0.5) * fraction * fraction,
    )


def stencil_table(cell, fraction, extent):
    weights = cubic_weights(fraction)
    position = lax.broadcasted_iota(jnp.int32, (extent, cell.shape[1]), 0)
    table = jnp.zeros((extent, cell.shape[1]), F32)
    for offset in range(4):
        target = cell + (offset - 1)
        target = jnp.where(target < 0, extent - 1, target)
        table = jnp.where(position == target, weights[offset], table)
    return table


def halves(value):
    high = value.astype(BF16)
    return high, (value - high.astype(F32)).astype(BF16)


def dot_pieces(left, right, dims=(((1,), (0,)), ((), ()))):
    dot = functools.partial(lax.dot_general, dimension_numbers=dims, preferred_element_type=F32)
    return dot(left[0], right[0]) + (dot(left[0], right[1]) + dot(left[1], right[0]))


def add(a, b):
    return (a[0] + b[0], a[1] + b[1])


def sub(a, b):
    return (a[0] - b[0], a[1] - b[1])


def quarter(a, sign):
    return (-sign * a[1], sign * a[0])


def dft4(x, sign):
    p, m = add(x[0], x[2]), sub(x[0], x[2])
    q, n = add(x[1], x[3]), quarter(sub(x[1], x[3]), sign)
    return [add(p, q), add(m, n), sub(p, q), sub(m, n)]


def dft8(x, sign):
    even, odd = dft4(x[0::2], sign), dft4(x[1::2], sign)
    r = math.sqrt(0.5)
    a, c = odd[1], odd[3]
    odd = [
        odd[0],
        (r * (a[0] - sign * a[1]), r * (a[1] + sign * a[0])),
        quarter(odd[2], sign),
        (r * (-c[0] - sign * c[1]), r * (-c[1] + sign * c[0])),
    ]
    return [add(e, o) for e, o in zip(even, odd)] + [sub(e, o) for e, o in zip(even, odd)]


def spread_kernel(vec, rows, cols, frac, trig_hi, trig_lo, twist, *rest):
    outs, (field, mixed) = rest[:PARTS], rest[PARTS:]
    tiles, ext = field.shape[1], field.shape[2]
    count = outs[0].shape[0]
    width = outs[0].shape[2] // 2
    share = count // RADIX
    field[...] = jnp.zeros_like(field)

    def one_tile(t, carry):
        row_tab = stencil_table(rows[pl.ds(t, 1), :], frac[0, pl.ds(t, 1), :], ext)
        col_tab = stencil_table(cols[pl.ds(t, 1), :], frac[1, pl.ds(t, 1), :], 2 * TC)
        weighted = jnp.concatenate(
            [row_tab * vec[0, pl.ds(t, 1), :], row_tab * vec[1, pl.ds(t, 1), :]], axis=0
        )
        piece = dot_pieces(halves(weighted), halves(col_tab), (((1,), (1,)), ((), ())))
        after = lax.rem(t + 1, tiles)
        before = lax.rem(t + tiles - 1, tiles)
        low = lax.broadcasted_iota(jnp.int32, (ext, TC), 1) < TC // 2
        for k in range(2):
            block = piece[k * ext : (k + 1) * ext]
            rim = block[:, TC:]
            field[k, t] = field[k, t] + block[:, :TC]
            field[k, after] = field[k, after] + jnp.where(low, rim, 0.0)
            field[k, before] = field[k, before] + jnp.where(low, 0.0, rim)
        return carry

    lax.fori_loop(0, tiles, one_tile, 0)

    def one_strip(i, carry):
        strip = pl.ds(pl.multiple_of(i * 8, 8), 8)
        for h in range(LONG // TC):
            lanes = slice(h * TC, (h + 1) * TC)
            x = [
                (field[0, j * (LONG // TC) + h, strip, :], field[1, j * (LONG // TC) + h, strip, :])
                for j in range(RADIX)
            ]
            for d, (re, im) in enumerate(dft8(x, -1.0)):
                c = twist[d : d + 1, lanes]
                s = twist[RADIX + d : RADIX + d + 1, lanes]
                mixed[d, 0, strip, lanes] = re * c - im * s
                mixed[d, 1, strip, lanes] = re * s + im * c
        return carry

    lax.fori_loop(0, ext // 8, one_strip, 0)
    table = (trig_hi[...], trig_lo[...])
    for d in range(RADIX):
        x = jnp.concatenate([mixed[d, 0], mixed[d, 1]], axis=0)
        y = dot_pieces(halves(x), table)
        re = y[:ext, :LONG] - y[ext:, LONG:]
        im = y[ext:, :LONG] + y[:ext, LONG:]
        for i in range(share):
            for h in range(PARTS):
                start = (i * PARTS + h) * width
                outs[h][d * share + i, :, :width] = re[:, start : start + width]
                outs[h][d * share + i, :, width:] = im[:, start : start + width]


def middle_kernel(part, ext_in, spectrum, trig_hi, trig_lo, twist, ext_out, grid, mixed):
    count, ext, both = ext_in.shape
    width = both // 2
    rows = ext - RIM
    for s in range(count):
        grid[s * rows : (s + 1) * rows] = ext_in[s, :rows]
    upper = lax.broadcasted_iota(jnp.int32, (RIM, both), 0) < RIM // 2
    for s in range(count):
        rim = ext_in[s, rows:]
        after = (s + 1) % count * rows
        before = ((s + count - 1) % count + 1) * rows - RIM
        grid[after : after + RIM] = grid[after : after + RIM] + jnp.where(upper, rim, 0.0)
        grid[before : before + RIM] = grid[before : before + RIM] + jnp.where(upper, 0.0, rim)

    def forward(i, carry):
        start = pl.multiple_of(i * 8, 8)
        x = []
        for j in range(RADIX):
            strip = pl.ds(pl.multiple_of(j * LONG + start, 8), 8)
            x.append((grid[strip, :width], grid[strip, width:]))
        for e, (re, im) in enumerate(dft8(x, -1.0)):
            c = twist[pl.ds(start, 8), e : e + 1]
            s = twist[pl.ds(start, 8), RADIX + e : RADIX + e + 1]
            mixed[e, pl.ds(start, 8), :width] = re * c - im * s
            mixed[e, pl.ds(start, 8), width:] = re * s + im * c
        return carry

    lax.fori_loop(0, LONG // 8, forward, 0)
    table = (trig_hi[...], trig_lo[...])
    scale = 1.0 / (G * G)
    for e in range(RADIX):
        y = dot_pieces(table, halves(mixed[e]))
        factor = spectrum[e, :, part * width : (part + 1) * width] * scale
        re = (y[:LONG, :width] - y[LONG:, width:]) * factor
        im = (y[:LONG, width:] + y[LONG:, :width]) * factor
        y = dot_pieces(table, halves(jnp.concatenate([re, im], axis=1)))
        re = y[:LONG, :width] + y[LONG:, width:]
        im = y[:LONG, width:] - y[LONG:, :width]
        c = twist[:, e : e + 1]
        s = twist[:, RADIX + e : RADIX + e + 1]
        mixed[e, :, :width] = re * c + im * s
        mixed[e, :, width:] = im * c - re * s

    def backward(i, carry):
        start = pl.multiple_of(i * 8, 8)
        strip = pl.ds(start, 8)
        x = [(mixed[e, strip, :width], mixed[e, strip, width:]) for e in range(RADIX)]
        for j, (re, im) in enumerate(dft8(x, 1.0)):
            out = pl.ds(pl.multiple_of(j * LONG + start, 8), 8)
            grid[out, :width] = re
            grid[out, width:] = im
        return carry

    lax.fori_loop(0, LONG // 8, backward, 0)
    for s in range(count):
        ext_out[s, :rows] = grid[s * rows : (s + 1) * rows]
        after = (s + 1) % count * rows
        before = ((s + count - 1) % count + 1) * rows - RIM
        ext_out[s, rows:] = jnp.where(
            upper, grid[after : after + RIM], grid[before : before + RIM]
        )


def gather_kernel(rows, cols, frac, trig_hi, trig_lo, twist, *rest):
    ins, out, (field, mixed) = rest[:PARTS], rest[PARTS], rest[PARTS + 1 :]
    tiles, ext = field.shape[1], field.shape[2]
    count = ins[0].shape[0]
    width = ins[0].shape[2] // 2
    share = count // RADIX
    table = (trig_hi[...], trig_lo[...])
    for d in range(RADIX):
        blocks = [(d * share + i, h) for i in range(share) for h in range(PARTS)]
        re = jnp.concatenate([ins[h][b, :, :width] for b, h in blocks], axis=1)
        im = jnp.concatenate([ins[h][b, :, width:] for b, h in blocks], axis=1)
        y = dot_pieces(halves(jnp.concatenate([re, im], axis=0)), table)
        re = y[:ext, :LONG] + y[ext:, LONG:]
        im = y[ext:, :LONG] - y[:ext, LONG:]
        c = twist[d : d + 1, :]
        s = twist[RADIX + d : RADIX + d + 1, :]
        mixed[d, 0] = re * c + im * s
        mixed[d, 1] = im * c - re * s

    def one_strip(i, carry):
        strip = pl.ds(pl.multiple_of(i * 8, 8), 8)
        for h in range(LONG // TC):
            lanes = slice(h * TC, (h + 1) * TC)
            x = [(mixed[d, 0, strip, lanes], mixed[d, 1, strip, lanes]) for d in range(RADIX)]
            for j, (re, im) in enumerate(dft8(x, 1.0)):
                field[0, j * (LONG // TC) + h, strip, :] = re
                field[1, j * (LONG // TC) + h, strip, :] = im
        return carry

    lax.fori_loop(0, ext // 8, one_strip, 0)

    def one_tile(t, carry):
        row_tab = stencil_table(rows[pl.ds(t, 1), :], frac[0, pl.ds(t, 1), :], ext)
        col_tab = stencil_table(cols[pl.ds(t, 1), :], frac[1, pl.ds(t, 1), :], 2 * TC)
        after = lax.rem(t + 1, tiles)
        before = lax.rem(t + tiles - 1, tiles)
        low = lax.broadcasted_iota(jnp.int32, (ext, TC), 1) < TC // 2
        near = jnp.concatenate(
            [
                jnp.concatenate(
                    [field[k, t], jnp.where(low, field[k, after], field[k, before])], axis=1
                )
                for k in range(2)
            ],
            axis=0,
        )
        blended = dot_pieces(halves(near), halves(col_tab))
        for k in range(2):
            value = jnp.sum(row_tab * blended[k * ext : (k + 1) * ext], axis=0, keepdims=True)
            out[k, pl.ds(t, 1), :] = value
        return carry

    lax.fori_loop(0, tiles, one_tile, 0)


def split_table(table):
    high = table.astype(np.float32).astype(BF16)
    low = (table - high.astype(np.float64)).astype(np.float32).astype(BF16)
    return jnp.asarray(high), jnp.asarray(low)


def column_order(share, count, ranks, width):
    kept = width // (RADIX * share)
    order = [
        (width // RADIX) * (ranks * s + r) + i * kept + k
        for i in range(share)
        for r in range(ranks)
        for s in range(count)
        for k in range(kept)
    ]
    return np.array(order)


def exchanged_spectrum(spectrum, count, ranks):
    share = count // RADIX
    width = spectrum.shape[1]
    late = width % (RADIX * share) == 0
    if not late:
        spectrum = lax.all_gather(spectrum, "rhs", axis=1, tiled=True)
        width = spectrum.shape[1]
        ranks = 1
    kept = width // (RADIX * share)
    turned = spectrum.T.reshape(share, kept, RADIX, G).transpose(2, 0, 1, 3)
    turned = lax.all_to_all(turned.reshape(count, kept, G), "slab", 0, 0, tiled=True)
    turned = turned.reshape(count * kept, G)
    if late:
        turned = lax.all_gather(turned, "rhs", axis=0, tiled=True)
    by_residue = turned.T.reshape(LONG, RADIX, -1).transpose(1, 0, 2)
    return by_residue, column_order(share, count, ranks, width)


def meet(me, rank, count):
    barrier = pltpu.get_barrier_semaphore()
    for step in range(1, count):
        pl.semaphore_signal(
            barrier,
            inc=1,
            device_id=(lax.rem(me + step, count), rank),
            device_id_type=pl.DeviceIdType.MESH,
        )
    pl.semaphore_wait(barrier, count - 1)


def exchange_kernel(sent, got, send_sems, recv_sems, own_sem):
    me, rank = lax.axis_index("slab"), lax.axis_index("rhs")
    count = sent.shape[0]
    meet(me, rank, count)
    copies = []
    for step in range(1, count):
        peer = lax.rem(me + step, count)
        copy = pltpu.make_async_remote_copy(
            src_ref=sent.at[peer],
            dst_ref=got.at[me],
            send_sem=send_sems.at[step],
            recv_sem=recv_sems.at[step],
            device_id=(peer, rank),
            device_id_type=pl.DeviceIdType.MESH,
        )
        copy.start()
        copies.append(copy)
    own = pltpu.make_async_copy(sent.at[me], got.at[me], own_sem)
    own.start()
    own.wait()
    for copy in copies:
        copy.wait()


def exchanged(blocks):
    count = blocks.shape[0]
    return pl.pallas_call(
        exchange_kernel,
        out_shape=jax.ShapeDtypeStruct(blocks.shape, blocks.dtype),
        in_specs=[pl.BlockSpec(memory_space=pl.ANY)],
        out_specs=pl.BlockSpec(memory_space=pl.ANY),
        scratch_shapes=[
            pltpu.SemaphoreType.DMA((count,)),
            pltpu.SemaphoreType.DMA((count,)),
            pltpu.SemaphoreType.DMA,
        ],
        compiler_params=pltpu.CompilerParams(collective_id=0, has_side_effects=True),
        name="exchange",
    )(blocks)


def total_kernel(mine, out, all_parts, send_sems, recv_sems):
    me, rank = lax.axis_index("slab"), lax.axis_index("rhs")
    count = all_parts.shape[0]
    meet(me, rank, count)
    copies = []
    for step in range(1, count):
        copy = pltpu.make_async_remote_copy(
            src_ref=mine,
            dst_ref=all_parts.at[me],
            send_sem=send_sems.at[step],
            recv_sem=recv_sems.at[step],
            device_id=(lax.rem(me + step, count), rank),
            device_id_type=pl.DeviceIdType.MESH,
        )
        copy.start()
        copies.append(copy)
    all_parts[me] = mine[...]
    for copy in copies:
        copy.wait()
    out[...] = jnp.sum(all_parts[...], axis=0)


def total(partial):
    count = lax.axis_size("slab")
    tile = (8, 128)
    mine = jnp.broadcast_to(jnp.pad(partial, (0, tile[0] - partial.shape[0]))[:, None], tile)
    summed = pl.pallas_call(
        total_kernel,
        out_shape=jax.ShapeDtypeStruct(tile, F32),
        in_specs=[pl.BlockSpec(memory_space=pltpu.VMEM)],
        out_specs=pl.BlockSpec(memory_space=pltpu.VMEM),
        scratch_shapes=[
            pltpu.VMEM((count, *tile), F32),
            pltpu.SemaphoreType.DMA((count,)),
            pltpu.SemaphoreType.DMA((count,)),
        ],
        compiler_params=pltpu.CompilerParams(collective_id=1, has_side_effects=True),
        name="total",
    )(mine)
    return summed[: partial.shape[0], 0]


def per_device(targets, counts, cell_rows, cell_cols, fractions, spectrum, noise_var):
    tiles, capacity = cell_rows.shape
    count = lax.axis_size("slab")
    ranks = lax.axis_size("rhs")
    rows_dev = G // count
    ext = rows_dev + RIM
    width = G // count // PARTS
    both = 2 * width
    block = jax.ShapeDtypeStruct((count, ext, both), F32)

    factors, order = exchanged_spectrum(spectrum, count, ranks)
    short = np.arange(LONG)
    angle = (short[:, None] * order[None, :] % LONG) * (2.0 * np.pi / LONG)
    forth = split_table(np.concatenate([np.cos(angle), -np.sin(angle)], axis=1))
    back = split_table(np.concatenate([np.cos(angle).T, -np.sin(angle).T], axis=1))
    angle = (short[:, None] * short[None, :] % LONG) * (2.0 * np.pi / LONG)
    inner = split_table(np.concatenate([np.cos(angle), -np.sin(angle)], axis=0))
    angle = np.arange(RADIX)[:, None] * short[None, :] * (2.0 * np.pi / G)
    twist = np.concatenate([np.cos(angle), -np.sin(angle)], axis=0).astype(np.float32)
    twist_rows, twist_cols = jnp.asarray(twist.T), jnp.asarray(twist)
    scratch = [
        pltpu.VMEM((2, tiles, ext, TC), F32),
        pltpu.VMEM((RADIX, 2, ext, LONG), F32),
    ]

    slot_index = lax.broadcasted_iota(jnp.int32, (tiles, capacity), 1)
    live = (slot_index < counts[:, None]).astype(F32)

    def smoothed(direction):
        sent = pl.pallas_call(
            spread_kernel, out_shape=[block] * PARTS, scratch_shapes=scratch, name="spread"
        )(direction, cell_rows, cell_cols, fractions, *forth, twist_cols)
        returned = []
        for part in range(PARTS):
            there = exchanged(sent[part])
            weighed = pl.pallas_call(
                functools.partial(middle_kernel, part),
                out_shape=block,
                scratch_shapes=[
                    pltpu.VMEM((G, both), F32),
                    pltpu.VMEM((RADIX, LONG, both), F32),
                ],
                name="middle",
            )(there, factors, *inner, twist_rows)
            returned.append(exchanged(weighed))
        return pl.pallas_call(
            gather_kernel,
            out_shape=jax.ShapeDtypeStruct(direction.shape, F32),
            scratch_shapes=scratch,
            name="gather",
        )(cell_rows, cell_cols, fractions, *back, twist_cols, *returned)

    residual = live[None] * targets
    solution = jnp.zeros(residual.shape, F32)
    direction = residual
    norm_now = total(jnp.sum(residual * residual, axis=(1, 2)))
    for repeat in range(ITERS):
        image = live[None] * smoothed(direction) + noise_var[0] * direction
        product = total(jnp.sum(direction * image, axis=(1, 2)))
        alpha = (norm_now / product)[:, None, None]
        solution = solution + alpha * direction
        residual = residual - alpha * image
        if repeat + 1 < ITERS:
            norm_next = total(jnp.sum(residual * residual, axis=(1, 2)))
            direction = residual + (norm_next / norm_now)[:, None, None] * direction
            norm_now = norm_next
    return (solution, residual)


def solution(mesh):
    placed = (
        P("rhs", "slab", None),
        P("slab"),
        P("slab", None),
        P("slab", None),
        P(None, "slab", None),
        P(None, ("slab", "rhs")),
        P(),
    )
    return jax.shard_map(
        per_device,
        mesh=mesh,
        in_specs=placed,
        out_specs=(P("rhs", "slab", None), P("rhs", "slab", None)),
        check_vma=False,
    )
```

profile of v0, /device:TPU:5, one launch (start us, length us, event | category | flops | bytes accessed | tf_op | source)
XLA Modules:
  0.0 561.9 jit_solution(17734312044994780205)
XLA Ops:
  7.2 1.4 copy.22
  8.6 19.1 %all_to_all.5 = f32[8,8,2048]{2,1,0:T(8,128)} all-to-all(f32[8,8,2048]{2,1,0:T(8,128)S(1)} %copy.22), channel_id=1, replica_groups=mesh['slab'=8,'rhs'=4] {'slab'}, dimensions={0} | all-to-all | bytes 1048576 | tf_op jit(solution)/shard_map/all_to_all | solution.py:287
  28.3 0.7 fusion
  29.1 1.4 broadcast_multiply_fusion.vec
  30.5 17.1 %spread.2.sent = f32[8,264,512]{2,1,0:T(8,128)} custom-call(f32[2,16,256]{2,1,0:T(8,128)} %broadcast_multiply_fusion.vec, s32[16,256]{1,0:T(8,128)} %rows.7, s32[16,256]{1,0:T(8,128)} %cols.7, f32[2,16,256]{2,1,0:T(8,128)} %frac.7, bf16[256,512]{1,0:T(8,128)(2,1)} %constant.20.clone.trig_hi, bf16[256,512]{1,0:T(8,128)(2,1)} %constant.21.clone.trig_lo, ...), custom_call_target="tpu_custom_call" | custom-call | tf_op jit(solution)/shard_map/spread/pallas_call | solution.py:419
  47.5 71.9 %exchange.4.ext_in = f32[8,264,512]{2,1,0:T(8,128)} custom-call(f32[8,264,512]{2,1,0:T(8,128)} %spread.2.sent), custom_call_target="tpu_custom_call" | custom-call | tf_op jit(solution)/shard_map/exchange/pallas_call | solution.py:333
  119.4 1.9 copy.23
  121.4 2.0 copy.26
  123.4 17.3 %middle.2.sent = f32[8,264,512]{2,1,0:T(8,128)} custom-call(f32[8,264,512]{2,1,0:T(8,128)} %exchange.4.ext_in, f32[8,256,256]{2,1,0:T(8,128)} %bitcast.19, bf16[512,256]{1,0:T(8,128)(2,1)} %constant.24.clone.trig_hi, bf16[512,256]{1,0:T(8,128)(2,1)} %constant.25.clone.trig_lo, f32[256,16]{1,0:T(8,128)} %constant.26.clone.twist), custom_call_target="tpu_custom_call" | custom-call | tf_op jit(solution)/shard_map/middle/pallas_call | solution.py:425
  140.7 95.3 %exchange.5.rest_0_ = f32[8,264,512]{2,1,0:T(8,128)} custom-call(f32[8,264,512]{2,1,0:T(8,128)} %middle.2.sent), custom_call_target="tpu_custom_call" | custom-call | tf_op jit(solution)/shard_map/exchange/pallas_call | solution.py:333
  236.0 15.4 %gather.2 = f32[2,16,256]{2,1,0:T(8,128)} custom-call(s32[16,256]{1,0:T(8,128)} %rows.7, s32[16,256]{1,0:T(8,128)} %cols.7, f32[2,16,256]{2,1,0:T(8,128)} %frac.7, bf16[256,512]{1,0:T(8,128)(2,1)} %constant.22.clone.trig_hi, bf16[256,512]{1,0:T(8,128)(2,1)} %constant.23.clone.trig_lo, f32[16,256]{1,0:T(8,128)} %constant.27.clone.twist, ...), custom_call_target="tpu_custom_call" | custom-call | tf_op jit(solution)/shard_map/gather/pallas_call | solution.py:435
  251.5 0.9 multiply_reduce_fusion.3
  252.4 0.7 broadcast_in_dim.9.mine
  253.0 31.4 %total.5 = f32[8,128]{1,0:T(8,128)} custom-call(f32[8,128]{1,0:T(8,128)} %broadcast_in_dim.9.mine), custom_call_target="tpu_custom_call" | custom-call | tf_op jit(solution)/shard_map/total/pallas_call | solution.py:374
  284.5 0.7 broadcast_in_dim.8.mine
  285.1 6.6 %total.4 = f32[8,128]{1,0:T(8,128)} custom-call(f32[8,128]{1,0:T(8,128)} %broadcast_in_dim.8.mine), custom_call_target="tpu_custom_call" | custom-call | tf_op jit(solution)/shard_map/total/pallas_call | solution.py:374
  291.8 0.8 fusion.1
  292.6 0.9 multiply_reduce_fusion.1
  293.5 0.7 broadcast_in_dim.10.mine
  294.2 6.6 %total.6 = f32[8,128]{1,0:T(8,128)} custom-call(f32[8,128]{1,0:T(8,128)} %broadcast_in_dim.10.mine), custom_call_target="tpu_custom_call" | custom-call | tf_op jit(solution)/shard_map/total/pallas_call | solution.py:374
  300.8 0.8 divide_reduce_fusion
  301.6 1.5 multiply_add_fusion.2.vec
  303.1 17.1 %spread.3.sent = f32[8,264,512]{2,1,0:T(8,128)} custom-call(f32[2,16,256]{2,1,0:T(8,128)} %multiply_add_fusion.2.vec, s32[16,256]{1,0:T(8,128)} %rows.7, s32[16,256]{1,0:T(8,128)} %cols.7, f32[2,16,256]{2,1,0:T(8,128)} %frac.7, bf16[256,512]{1,0:T(8,128)(2,1)} %constant.20.clone.trig_hi, bf16[256,512]{1,0:T(8,128)(2,1)} %constant.21.clone.trig_lo, ...), custom_call_target="tpu_custom_call" | custom-call | tf_op jit(solution)/shard_map/spread/pallas_call | solution.py:419
  320.2 66.7 %exchange.6.ext_in = f32[8,264,512]{2,1,0:T(8,128)} custom-call(f32[8,264,512]{2,1,0:T(8,128)} %spread.3.sent), custom_call_target="tpu_custom_call" | custom-call | tf_op jit(solution)/shard_map/exchange/pallas_call | solution.py:333
  386.9 17.3 %middle.3.sent = f32[8,264,512]{2,1,0:T(8,128)} custom-call(f32[8,264,512]{2,1,0:T(8,128)} %exchange.6.ext_in, f32[8,256,256]{2,1,0:T(8,128)} %bitcast.20, bf16[512,256]{1,0:T(8,128)(2,1)} %constant.24.clone.trig_hi, bf16[512,256]{1,0:T(8,128)(2,1)} %constant.25.clone.trig_lo, f32[256,16]{1,0:T(8,128)} %constant.26.clone.twist), custom_call_target="tpu_custom_call" | custom-call | tf_op jit(solution)/shard_map/middle/pallas_call | solution.py:425
  404.2 98.3 %exchange.7.rest_0_ = f32[8,264,512]{2,1,0:T(8,128)} custom-call(f32[8,264,512]{2,1,0:T(8,128)} %middle.3.sent), custom_call_target="tpu_custom_call" | custom-call | tf_op jit(solution)/shard_map/exchange/pallas_call | solution.py:333
  502.6 15.4 %gather.3 = f32[2,16,256]{2,1,0:T(8,128)} custom-call(s32[16,256]{1,0:T(8,128)} %rows.7, s32[16,256]{1,0:T(8,128)} %cols.7, f32[2,16,256]{2,1,0:T(8,128)} %frac.7, bf16[256,512]{1,0:T(8,128)(2,1)} %constant.22.clone.trig_hi, bf16[256,512]{1,0:T(8,128)(2,1)} %constant.23.clone.trig_lo, f32[16,256]{1,0:T(8,128)} %constant.27.clone.twist, ...), custom_call_target="tpu_custom_call" | custom-call | tf_op jit(solution)/shard_map/gather/pallas_call | solution.py:435
  518.0 0.9 multiply_reduce_fusion
  518.9 0.7 broadcast_in_dim.11.mine
  519.5 33.2 %total.7 = f32[8,128]{1,0:T(8,128)} custom-call(f32[8,128]{1,0:T(8,128)} %broadcast_in_dim.11.mine), custom_call_target="tpu_custom_call" | custom-call | tf_op jit(solution)/shard_map/total/pallas_call | solution.py:374
  552.8 0.8 fusion.2
  553.6 1.5 multiply_subtract_fusion
  (13 shorter events, 0.1 us)
Async XLA Ops:
  7.2 112.3 %all-gather.2.cloned.1.call-start = ((), (), s32[]{:S(2)}) async-start(), calls=%async_computation.1 | async-start | bytes 2621440 | tf_op jit(solution)/shard_map/all_gather | solution.py:290
  236.0 15.5 %copy-start.1 = (f32[2,16,256]{2,1,0:T(8,128)S(1)}, f32[2,16,256]{2,1,0:T(8,128)}, u32[]{:S(2)}) copy-start(f32[2,16,256]{2,1,0:T(8,128)} %param.15) | copy-start | bytes 98308
  502.5 15.5 %copy-start.2 = (f32[2,16,256]{2,1,0:T(8,128)S(1)}, f32[2,16,256]{2,1,0:T(8,128)}, u32[]{:S(2)}) copy-start(f32[2,16,256]{2,1,0:T(8,128)} %multiply_add_fusion.2.vec) | copy-start | bytes 98308
  502.6 51.0 %copy-start = (f32[2,16,256]{2,1,0:T(8,128)S(1)}, f32[2,16,256]{2,1,0:T(8,128)}, u32[]{:S(2)}) copy-start(f32[2,16,256]{2,1,0:T(8,128)} %gather.2) | copy-start | bytes 98308
Sparse Core Ops, SparseCore 0:
  27.8 21.9 all-gather.1
where the time goes:
time: 566 us; the launch traced here: 562 us
  Pallas kernels  510 us (90%)
  blocking collectives  19.1 us (3%)
  between operations  14.8 us (3%)
  other arithmetic  10.1 us (2%)
  local copies, waits for them, and re-layouts  7.98 us (1%)
    pallas_call x4, Pallas kernels, exchanged(): pl.pallas_call(exchange_kernel, out_shape=jax.ShapeDtypeStruct(blocks.sha...  332 us
    pallas_call x4, Pallas kernels, total(): pl.pallas_call(total_kernel, out_shape=jax.ShapeDtypeStruct(tile, F32), i...  77.9 us
    pallas_call x2, Pallas kernels, smoothed(): pl.pallas_call(functools.partial(middle_kernel, part), out_shape=block, s...  34.6 us
    pallas_call x2, Pallas kernels, smoothed(): pl.pallas_call(spread_kernel, out_shape=[block] * PARTS, scratch_shapes=s...  34.2 us
    pallas_call x2, Pallas kernels, smoothed(): pl.pallas_call(gather_kernel, out_shape=jax.ShapeDtypeStruct(direction.sh...  30.9 us
    all_to_all x1, blocking collectives, exchanged_spectrum(): lax.all_to_all(turned.reshape(count, kept, G), 'slab', 0, 0, tiled=True)  19.1 us
  transfers between devices with their start and end apart: 1, of which 0 were waited for; matrix products, arithmetic and copies ran while one was open for 0% of the time, Pallas kernels for 16%

commit v1 on v0

v1 whole, which is shorter than its diff:
```python
import functools
import math

import jax
import jax.numpy as jnp
import numpy as np
from jax import lax
from jax.experimental import pallas as pl
from jax.experimental.pallas import tpu as pltpu
from jax.sharding import PartitionSpec as P

G = 2048
TC = 128
ITERS = 2
RADIX = 8
LONG = G // RADIX
RIM = 8
WIDE = TC + RIM
NOWHERE = 4 * G
F32 = jnp.float32
BF16 = jnp.bfloat16
NT = (((1,), (1,)), ((), ()))
MESH = pl.DeviceIdType.MESH


def cubic_weights(fraction):
    return (
        ((-0.5 * fraction + 1.0) * fraction - 0.5) * fraction,
        (1.5 * fraction - 2.5) * fraction * fraction + 1.0,
        ((-1.5 * fraction + 2.0) * fraction + 0.5) * fraction,
        (0.5 * fraction - 0.5) * fraction * fraction,
    )


def stencil_table(cell, fraction, extent):
    weights = cubic_weights(fraction)
    position = lax.broadcasted_iota(jnp.int32, (extent, cell.shape[1]), 0)
    table = jnp.zeros((extent, cell.shape[1]), F32)
    for offset in range(4):
        target = cell + (offset - 1)
        target = jnp.where(target < 0, extent - 1, target)
        table = jnp.where(position == target, weights[offset], table)
    return table


def halves(value):
    high = value.astype(BF16)
    return high, (value - high.astype(F32)).astype(BF16)


def dot_pieces(left, right, dims=(((1,), (0,)), ((), ()))):
    dot = functools.partial(lax.dot_general, dimension_numbers=dims, preferred_element_type=F32)
    return dot(left[0], right[0]) + (dot(left[0], right[1]) + dot(left[1], right[0]))


def add(a, b):
    return (a[0] + b[0], a[1] + b[1])


def sub(a, b):
    return (a[0] - b[0], a[1] - b[1])


def quarter(a, sign):
    return (-sign * a[1], sign * a[0])


def dft4(x, sign):
    p, m = add(x[0], x[2]), sub(x[0], x[2])
    q, n = add(x[1], x[3]), quarter(sub(x[1], x[3]), sign)
    return [add(p, q), add(m, n), sub(p, q), sub(m, n)]


def dft8(x, sign):
    even, odd = dft4(x[0::2], sign), dft4(x[1::2], sign)
    r = math.sqrt(0.5)
    a, c = odd[1], odd[3]
    odd = [
        odd[0],
        (r * (a[0] - sign * a[1]), r * (a[1] + sign * a[0])),
        quarter(odd[2], sign),
        (r * (-c[0] - sign * c[1]), r * (-c[1] + sign * c[0])),
    ]
    return [add(e, o) for e, o in zip(even, odd)] + [sub(e, o) for e, o in zip(even, odd)]


class Place:
    def __init__(self):
        self.slabs, self.ranks = lax.axis_size("slab"), lax.axis_size("rhs")
        self.slab, self.rank = lax.axis_index("slab"), lax.axis_index("rhs")
        self.deep = self.slabs // self.ranks
        self.pairs = self.ranks // 2
        self.blocks = self.slabs // 2
        self.classes = self.deep * self.pairs
        self.half = lax.rem(self.rank, 2)
        self.field = lax.div(self.slab, self.deep)
        self.own_class = lax.rem(self.slab, self.deep) * self.pairs + lax.div(self.rank, 2)

    def member(self, field, own_class, half):
        slab = field * self.deep + own_class // self.pairs
        return slab, 2 * (own_class % self.pairs) + half

    def is_me(self, slab, rank):
        return jnp.logical_and(slab == self.slab, rank == self.rank)


def greet(senders, expected):
    barrier = pltpu.get_barrier_semaphore()
    for device, mine in senders:
        if mine is None:
            pl.semaphore_signal(barrier, inc=1, device_id=device, device_id_type=MESH)
        else:

            @pl.when(jnp.logical_not(mine))
            def _(device=device):
                pl.semaphore_signal(barrier, inc=1, device_id=device, device_id_type=MESH)

    pl.semaphore_wait(barrier, expected)


def remote(src, dst, send_sem, recv_sem, device):
    return pltpu.make_async_remote_copy(
        src_ref=src,
        dst_ref=dst,
        send_sem=send_sem,
        recv_sem=recv_sem,
        device_id=device,
        device_id_type=MESH,
    )


def turn_kernel(spectrum, pieces, turned):
    classes, _, kept, _ = pieces.shape
    for d in range(RADIX):
        strided = spectrum[pl.ds(d, LONG, stride=RADIX), :]
        for h in range(LONG // TC):
            turned[h] = strided[h * TC : (h + 1) * TC].T
            for w in range(classes):
                pieces[w, d, :, h * TC : (h + 1) * TC] = turned[h, pl.ds(w, kept, stride=classes), :]


def collect_kernel(with_pieces, *refs):
    if with_pieces:
        stat, targ, pieces, statg, targg, gotp, *sems = refs
    else:
        stat, targ, statg, targg, *sems = refs
    stat_send, stat_recv, targ_send, targ_recv, piece_send, piece_recv, own_sem = sems
    at = Place()
    towards = lax.div(at.slab, at.blocks)
    spot = lax.rem(at.slab, at.blocks)
    base = 2 * lax.div(at.rank, 2)
    parity = lax.rem(at.rank, 2)
    stat_to = [(2 * i + parity, base + towards) for i in range(at.slabs // 2)]
    targ_to = [at.member(at.rank, i, towards) for i in range(at.classes)]
    first = at.half * at.blocks
    stat_from = [(first + b, base + lax.rem(at.slab, 2)) for b in range(at.blocks)]
    targ_from = [(first + b, at.field) for b in range(at.blocks)]
    index = lax.rem(at.slab, at.deep) * at.ranks + at.rank
    peers = []
    if with_pieces:
        for step in range(1, at.slabs):
            other = lax.rem(index + step, at.slabs)
            peers.append((at.field * at.deep + other // at.ranks, other % at.ranks))
    senders = [(d, at.is_me(*d)) for d in stat_from + targ_from] + [(d, None) for d in peers]
    expected = len(peers)
    for device in stat_to + targ_to:
        expected = expected + jnp.where(at.is_me(*device), 0, 1)
    greet(senders, expected)

    for src, dst, goals, send, recv in (
        (stat, statg, stat_to, stat_send, stat_recv),
        (targ, targg, targ_to, targ_send, targ_recv),
    ):
        for i, device in enumerate(goals):
            same = at.is_me(*device)

            @pl.when(jnp.logical_not(same))
            def _(src=src, dst=dst, send=send, recv=recv, i=i, device=device):
                remote(src, dst.at[spot], send.at[i], recv.at[spot], device).start()

            @pl.when(same)
            def _(src=src, dst=dst, recv=recv):
                pltpu.make_async_copy(src, dst.at[spot], recv.at[spot]).start()

    copies = []
    if with_pieces:
        for step, (slab, rank) in enumerate(peers, 1):
            wanted = at.classes * (rank % 2) + (slab % at.deep) * at.pairs + rank // 2
            copy = remote(
                pieces.at[wanted], gotp.at[index], piece_send.at[step], piece_recv.at[step], (slab, rank)
            )
            copy.start()
            copies.append(copy)
        own = pltpu.make_async_copy(
            pieces.at[at.classes * at.half + at.own_class], gotp.at[index], own_sem
        )
        own.start()
        own.wait()

    for src, dst, goals, sources, send, recv in (
        (stat, statg, stat_to, stat_from, stat_send, stat_recv),
        (targ, targg, targ_to, targ_from, targ_send, targ_recv),
    ):
        for i, device in enumerate(goals):

            @pl.when(jnp.logical_not(at.is_me(*device)))
            def _(src=src, dst=dst, send=send, recv=recv, i=i, device=device):
                remote(src, dst.at[spot], send.at[i], recv.at[spot], device).wait_send()

        for b, device in enumerate(sources):
            same = at.is_me(*device)

            @pl.when(jnp.logical_not(same))
            def _(src=src, dst=dst, send=send, recv=recv, b=b, device=device):
                remote(src, dst.at[b], send.at[0], recv.at[b], device).wait_recv()

            @pl.when(same)
            def _(src=src, dst=dst, recv=recv, b=b):
                pltpu.make_async_copy(src, dst.at[b], recv.at[b]).wait()

    for copy in copies:
        copy.wait()


def pair_kernel(main, rim, got_main, got_rim, send_sems, recv_sems):
    at = Place()
    partner = (at.slab, at.rank + 1 - 2 * at.half)
    greet([(partner, None)], 1)
    copies = [
        remote(main, got_main, send_sems.at[0], recv_sems.at[0], partner),
        remote(rim, got_rim, send_sems.at[1], recv_sems.at[1], partner),
    ]
    for copy in copies:
        copy.start()
    for copy in copies:
        copy.wait()


def spread_kernel(
    stat, vec, phases, tab_own, tab_oth, own, own_rim, oth, oth_rim, field, rims
):
    blocks, _, tiles, _ = stat.shape
    _, _, folds, _, rows = field.shape
    ext = rows + RIM
    long = tab_own.shape[1]
    half = tab_own.shape[0] // 2
    span = long // TC
    radix = folds // span

    def clear(b, carry):
        field[b] = jnp.zeros(field.shape[1:], F32)
        rims[b] = jnp.zeros(rims.shape[1:], F32)
        return carry

    lax.fori_loop(0, blocks, clear, 0)

    def one_tile(i, carry):
        b, t = lax.div(i, tiles), lax.rem(i, tiles)
        here = lax.rem(t, folds)
        after, before = lax.rem(t + 1, folds), lax.rem(t + folds - 1, folds)
        slot = [stat[b, j, pl.ds(t, 1), :] for j in range(4)]
        row_tab = stencil_table(slot[0].astype(jnp.int32), slot[2], ext)
        col_tab = stencil_table(slot[1].astype(jnp.int32), slot[3], WIDE)
        v0, v1 = vec[b, 0, pl.ds(t, 1), :], vec[b, 1, pl.ds(t, 1), :]
        part = lax.div(t, span)
        pr, pi = phases[0, part], phases[1, part]
        weighted = jnp.concatenate(
            [col_tab * (v0 * pr - v1 * pi), col_tab * (v0 * pi + v1 * pr)], axis=0
        )
        piece = dot_pieces(halves(weighted), halves(row_tab), NT)
        wr, wi = phases[0, 1], phases[1, 1]
        leave = lax.rem(t + 1, span) == 0
        enter = lax.rem(t, span) == 0
        ar, ai = jnp.where(leave, wr, 1.0), jnp.where(leave, wi, 0.0)
        br, bi = jnp.where(enter, wr, 1.0), jnp.where(enter, -wi, 0.0)
        re, im = piece[TC:WIDE], piece[WIDE + TC :]
        low = lax.broadcasted_iota(jnp.int32, (RIM, ext), 0) < RIM // 2
        ahead = (re * ar - im * ai, re * ai + im * ar)
        behind = (re * br - im * bi, re * bi + im * br)
        for k in range(2):
            block = piece[k * WIDE : k * WIDE + TC]
            field[b, k, here] = field[b, k, here] + block[:, :rows]
            rims[b, k, here] = rims[b, k, here] + block[:, rows:]
            edge = jnp.where(low, ahead[k], 0.0)
            field[b, k, after, :RIM] = field[b, k, after, :RIM] + edge[:, :rows]
            rims[b, k, after, :RIM] = rims[b, k, after, :RIM] + edge[:, rows:]
            edge = jnp.where(low, 0.0, behind[k])
            field[b, k, before, TC - RIM :] = field[b, k, before, TC - RIM :] + edge[:, :rows]
            rims[b, k, before, TC - RIM :] = rims[b, k, before, TC - RIM :] + edge[:, rows:]
        return carry

    lax.fori_loop(0, blocks * tiles, one_tile, 0)
    first = lax.broadcasted_iota(jnp.int32, (TC, RIM), 1) < RIM // 2

    def merge(i, carry):
        k, ft = lax.div(i, folds), lax.rem(i, folds)
        for b in range(blocks):
            rim = rims[b, k, ft]
            if b + 1 < blocks:
                up = field[b + 1, k, ft, :, :RIM]
                field[b + 1, k, ft, :, :RIM] = up + jnp.where(first, rim, 0.0)
            if b > 0:
                down = field[b - 1, k, ft, :, rows - RIM :]
                field[b - 1, k, ft, :, rows - RIM :] = down + jnp.where(first, 0.0, rim)
        rims[0, k, ft] = jnp.where(first, rims[blocks - 1, k, ft], rims[0, k, ft])
        return carry

    lax.fori_loop(0, 2 * folds, merge, 0)
    tables = (halves(tab_own[...]), halves(tab_oth[...]))
    sigma = phases[2, 0]

    def transform(load, width, outs):
        x = [
            jnp.concatenate([load(k, c * span, (c + 1) * span) for k in range(2)], axis=1)
            for c in range(radix)
        ]
        if radix == 2:
            turned = sigma * x[1]
            x = [x[0] + turned, x[0] - turned]
        else:
            x = [x[0], x[0]]
        for table, value, out in zip(tables, x, outs):
            y = dot_pieces(table, halves(value))
            out[0] = y[:half, :width] - y[half:, width:]
            out[1] = y[:half, width:] + y[half:, :width]

    def one_block(b, carry):
        load = lambda k, lo, hi: field[b, k, lo:hi].reshape(long, rows)
        transform(load, rows, (own.at[b], oth.at[b]))
        return carry

    lax.fori_loop(0, blocks, one_block, 0)
    pad = jnp.zeros((long, TC - RIM), F32)

    def load_rim(k, lo, hi):
        return jnp.concatenate([rims[0, k, lo:hi].reshape(long, RIM), pad], axis=1)

    transform(load_rim, TC, (own_rim, oth_rim))


def middle_kernel(
    own, own_rim, got, got_rim, spectrum, trig_hi, trig_lo, twist, keep, keep_rim, give, give_rim, mixed
):
    blocks, _, half, rows = own.shape
    groups = RADIX // 2
    per = LONG // rows
    chunks = LONG // TC
    narrow = TC // rows
    lane = lax.broadcasted_iota(jnp.int32, (8, TC), 1)

    def forward(i, carry):
        strip = pl.ds(pl.multiple_of(i * 8, 8), 8)
        for h in range(chunks):
            lanes = slice(h * TC, (h + 1) * TC)

            def fetch(j, k):
                src = own if j < groups else got
                spot = j % groups * per
                if narrow <= 1:
                    return src[spot, k, strip, lanes]
                return jnp.concatenate(
                    [src[spot + h * narrow + u, k, strip, :] for u in range(narrow)], axis=1
                )

            x = [[fetch(j, 0), fetch(j, 1)] for j in range(RADIX)]
            for k in range(2):
                mine, other = own_rim[k, strip, :], got_rim[k, strip, :]
                if h == 0:
                    x[groups][k] = x[groups][k] + jnp.where(lane < RIM // 2, mine, 0.0)
                    x[0][k] = x[0][k] + jnp.where(lane < RIM // 2, other, 0.0)
                if h == chunks - 1:
                    last = lane >= TC - RIM // 2
                    mine = pltpu.roll(mine, TC - RIM, 1)
                    other = pltpu.roll(other, TC - RIM, 1)
                    x[RADIX - 1][k] = x[RADIX - 1][k] + jnp.where(last, mine, 0.0)
                    x[groups - 1][k] = x[groups - 1][k] + jnp.where(last, other, 0.0)
            for d, (re, im) in enumerate(dft8([tuple(v) for v in x], -1.0)):
                c = twist[d : d + 1, lanes]
                s = twist[RADIX + d : RADIX + d + 1, lanes]
                mixed[d, 0, strip, lanes] = re * c - im * s
                mixed[d, 1, strip, lanes] = re * s + im * c
        return carry

    lax.fori_loop(0, half // 8, forward, 0)
    table = (trig_hi[...], trig_lo[...])
    scale = 1.0 / (G * G)
    for d in range(RADIX):
        x = jnp.concatenate([mixed[d, 0], mixed[d, 1]], axis=0)
        y = dot_pieces(halves(x), table)
        factor = spectrum[:, d].reshape(half, LONG) * scale
        re = (y[:half, :LONG] - y[half:, LONG:]) * factor
        im = (y[half:, :LONG] + y[:half, LONG:]) * factor
        y = dot_pieces(halves(jnp.concatenate([re, im], axis=0)), table)
        re = y[:half, :LONG] + y[half:, LONG:]
        im = y[half:, :LONG] - y[:half, LONG:]
        c = twist[d : d + 1, :]
        s = twist[RADIX + d : RADIX + d + 1, :]
        mixed[d, 0] = re * c + im * s
        mixed[d, 1] = im * c - re * s

    def backward(i, carry):
        strip = pl.ds(pl.multiple_of(i * 8, 8), 8)
        edges = {}
        for h in range(chunks):
            lanes = slice(h * TC, (h + 1) * TC)
            x = dft8([(mixed[d, 0, strip, lanes], mixed[d, 1, strip, lanes]) for d in range(RADIX)], 1.0)
            for j in range(RADIX):
                dst = keep if j < groups else give
                spot = j % groups * per
                for k in range(2):
                    if narrow <= 1:
                        dst[spot, k, strip, lanes] = x[j][k]
                    else:
                        for u in range(narrow):
                            dst[spot + h * narrow + u, k, strip, :] = x[j][k][:, u * rows : (u + 1) * rows]
            if h == 0:
                edges[0] = (x[groups], x[0])
            if h == chunks - 1:
                edges[1] = (x[RADIX - 1], x[groups - 1])
        for n, dst in enumerate((keep_rim, give_rim)):
            for k in range(2):
                tail = pltpu.roll(edges[1][n][k], RIM, 1)
                dst[k, strip, :] = jnp.where(lane < RIM // 2, edges[0][n][k], tail)
        return carry

    lax.fori_loop(0, half // 8, backward, 0)


def gather_kernel(
    stat, phases, tab_own, tab_oth, own, own_rim, got, got_rim, out, field, rims
):
    blocks, _, tiles, _ = stat.shape
    _, _, folds, _, rows = field.shape
    ext = rows + RIM
    long = tab_own.shape[0] // 2
    span = long // TC
    radix = folds // span
    tables = (halves(tab_own[...]), halves(tab_oth[...]))
    sigma = phases[2, 0]

    def transform(ins, width, store):
        u = []
        for table, value in zip(tables, ins):
            y = dot_pieces(table, halves(jnp.concatenate([value[0], value[1]], axis=1)))
            u.append((y[:long, :width] + y[long:, width:], y[:long, width:] - y[long:, :width]))
        total = [u[0][k] + u[1][k] for k in range(2)]
        for k in range(2):
            store(k, 0, total[k])
            if radix == 2:
                store(k, 1, sigma * (u[0][k] - u[1][k]))

    def one_block(b, carry):
        def store(k, c, value):
            field[b, k, c * span : (c + 1) * span] = value.reshape(span, TC, rows)

        transform((own.at[b], got.at[b]), rows, store)
        return carry

    lax.fori_loop(0, blocks, one_block, 0)
    first = lax.broadcasted_iota(jnp.int32, (TC, RIM), 1) < RIM // 2

    def store_rim(k, c, value):
        rims[blocks, k, c * span : (c + 1) * span] = value[:, :RIM].reshape(span, TC, RIM)

    transform((own_rim, got_rim), TC, store_rim)

    def near_rows(i, carry):
        k, ft = lax.div(i, folds), lax.rem(i, folds)
        for b in range(blocks):
            up = field[b + 1, k, ft, :, :RIM] if b + 1 < blocks else rims[blocks, k, ft]
            down = field[b - 1, k, ft, :, rows - RIM :] if b > 0 else rims[blocks, k, ft]
            rims[b, k, ft] = jnp.where(first, up, down)
        return carry

    lax.fori_loop(0, 2 * folds, near_rows, 0)

    def one_tile(i, carry):
        b, t = lax.div(i, tiles), lax.rem(i, tiles)
        here = lax.rem(t, folds)
        after, before = lax.rem(t + 1, folds), lax.rem(t + folds - 1, folds)
        slot = [stat[b, j, pl.ds(t, 1), :] for j in range(4)]
        row_tab = stencil_table(slot[0].astype(jnp.int32), slot[2], ext)
        col_tab = stencil_table(slot[1].astype(jnp.int32), slot[3], WIDE)
        part = lax.div(t, span)
        pr, pi = phases[0, part], phases[1, part]
        wr, wi = phases[0, 1], phases[1, 1]
        leave = lax.rem(t + 1, span) == 0
        enter = lax.rem(t, span) == 0
        ar, ai = jnp.where(leave, wr, 1.0), jnp.where(leave, -wi, 0.0)
        br, bi = jnp.where(enter, wr, 1.0), jnp.where(enter, wi, 0.0)

        def whole(k, ft, lo, hi):
            return jnp.concatenate([field[b, k, ft, lo:hi], rims[b, k, ft, lo:hi]], axis=1)

        nr, ni = whole(0, after, 0, RIM), whole(1, after, 0, RIM)
        lr, li = whole(0, before, TC - RIM, TC), whole(1, before, TC - RIM, TC)
        low = lax.broadcasted_iota(jnp.int32, (RIM, ext), 0) < RIM // 2
        edge = (
            jnp.where(low, nr * ar - ni * ai, lr * br - li * bi),
            jnp.where(low, nr * ai + ni * ar, lr * bi + li * br),
        )
        near = jnp.concatenate([whole(0, here, 0, TC), edge[0], whole(1, here, 0, TC), edge[1]], axis=0)
        blended = dot_pieces(halves(near), halves(row_tab))
        vr = jnp.sum(col_tab * blended[:WIDE], axis=0, keepdims=True)
        vi = jnp.sum(col_tab * blended[WIDE:], axis=0, keepdims=True)
        out[b, 0, pl.ds(t, 1), :] = vr * pr + vi * pi
        out[b, 1, pl.ds(t, 1), :] = vi * pr - vr * pi
        return carry

    lax.fori_loop(0, blocks * tiles, one_tile, 0)


def row_sums(values):
    row = lax.broadcasted_iota(jnp.int32, (8, TC), 0)
    tile = jnp.zeros((8, TC), F32)
    for i, value in enumerate(values):
        tile = jnp.where(row == i, value, tile)
    return tile


def full_sum(value):
    return jnp.sum(jnp.sum(value, axis=(0, 1)), keepdims=True).reshape(1, 1)


def update_kernel(
    last, partial, direction, residual, solution, noise, new_direction, new_residual, new_solution,
    parts, mine, got, send_sems, recv_sems, pair_send, pair_recv
):
    at = Place()
    partner = (at.slab, at.rank + 1 - 2 * at.half)
    peers = [
        at.member(at.field, lax.rem(at.own_class + step, at.classes), at.half)
        for step in range(1, at.classes)
    ]
    greet([(d, None) for d in peers] + [(partner, None)], len(peers) + 1)
    copies = []
    for step, device in enumerate(peers, 1):
        copy = remote(partial, parts.at[at.own_class], send_sems.at[step], recv_sems.at[step], device)
        copy.start()
        copies.append(copy)
    parts[at.own_class] = partial[...]
    for copy in copies:
        copy.wait()
    image = parts[0]
    for i in range(1, at.classes):
        image = image + parts[i]
    image = image + noise[0] * direction[...]

    def shared(n, values):
        mine[n] = row_sums(values)
        copy = remote(mine.at[n], got.at[n], pair_send.at[n], pair_recv.at[n], partner)
        copy.start()
        copy.wait()
        return mine[n] + got[n]

    new_residual[...] = image
    sums = []
    for k in range(2):
        sums.append(full_sum(residual[:, k] * residual[:, k]))
    for k in range(2):
        sums.append(full_sum(direction[:, k] * new_residual[:, k]))
    total = shared(0, sums)
    for k in range(2):
        alpha = total[k : k + 1, :1] / total[2 + k : 3 + k, :1]
        new_solution[:, k] = solution[:, k] + alpha * direction[:, k]
        new_residual[:, k] = residual[:, k] - alpha * new_residual[:, k]
    if last:
        new_direction[...] = jnp.zeros_like(new_direction)
        return
    again = shared(1, [full_sum(new_residual[:, k] * new_residual[:, k]) for k in range(2)])
    for k in range(2):
        beta = again[k : k + 1, :1] / total[k : k + 1, :1]
        new_direction[:, k] = new_residual[:, k] + beta * direction[:, k]


def deliver_kernel(solution, residual, out_solution, out_residual, send_sems, recv_sems):
    at = Place()
    goal = (at.half * at.blocks + at.own_class, at.field)
    source = at.member(at.rank, lax.rem(at.slab, at.blocks), lax.div(at.slab, at.blocks))
    same, from_me = at.is_me(*goal), at.is_me(*source)
    barrier = pltpu.get_barrier_semaphore()

    @pl.when(jnp.logical_not(from_me))
    def _():
        pl.semaphore_signal(barrier, inc=1, device_id=source, device_id_type=MESH)

    @pl.when(jnp.logical_not(same))
    def _():
        pl.semaphore_wait(barrier, 1)

    for n, (src, dst) in enumerate(((solution, out_solution), (residual, out_residual))):

        @pl.when(jnp.logical_not(same))
        def _(src=src, dst=dst, n=n):
            remote(src.at[at.own_class], dst, send_sems.at[n], recv_sems.at[n], goal).start()

        @pl.when(same)
        def _(src=src, dst=dst, n=n):
            pltpu.make_async_copy(src.at[at.own_class], dst, recv_sems.at[n]).start()

    for n, (src, dst) in enumerate(((solution, out_solution), (residual, out_residual))):

        @pl.when(jnp.logical_not(same))
        def _(src=src, dst=dst, n=n):
            remote(src.at[at.own_class], dst, send_sems.at[n], recv_sems.at[n], goal).wait()

        @pl.when(same)
        def _(src=src, dst=dst, n=n):
            pltpu.make_async_copy(src.at[at.own_class], dst, recv_sems.at[n]).wait()


def split_table(table):
    high = table.astype(np.float32).astype(BF16)
    low = (table - high.astype(np.float64)).astype(np.float32).astype(BF16)
    return jnp.asarray(high), jnp.asarray(low)


def shape_of(*shape):
    return jax.ShapeDtypeStruct(shape, F32)


def talk(kernel, out_shape, scratch, ident, name, space=pl.ANY, special=()):
    def call(*operands):
        specs = [pl.BlockSpec(memory_space=space)] * len(operands)
        for i in special:
            specs[i] = pl.BlockSpec(memory_space=pltpu.SMEM)
        return pl.pallas_call(
            kernel,
            out_shape=out_shape,
            in_specs=specs,
            out_specs=[pl.BlockSpec(memory_space=space)] * len(out_shape),
            scratch_shapes=scratch,
            compiler_params=pltpu.CompilerParams(collective_id=ident, has_side_effects=True),
            name=name,
        )(*operands)

    return call


def dma(*shape):
    return pltpu.SemaphoreType.DMA(shape)


def per_device(targets, counts, cell_rows, cell_cols, fractions, spectrum, noise_var):
    tiles, capacity = cell_rows.shape
    at = Place()
    slabs, ranks, blocks, classes = at.slabs, at.ranks, at.blocks, at.classes
    rows = G // slabs
    fold = G // classes
    long = min(LONG, fold)
    radix = fold // long
    half = fold // 2
    parts = G // long
    width = spectrum.shape[1]

    slot_index = lax.broadcasted_iota(jnp.int32, (tiles, capacity), 1)
    live = slot_index < counts[:, None]
    stat = jnp.stack(
        [
            jnp.where(live, cell_rows, NOWHERE).astype(F32),
            cell_cols.astype(F32),
            fractions[0],
            fractions[1],
        ]
    )
    targ = jnp.where(live[None], targets, 0.0)

    step = classes if radix == 2 else classes * half
    offsets = [at.own_class + step * at.half, at.own_class + step * (1 - at.half)]
    eighth = jnp.arange(parts, dtype=jnp.int32)
    angle = ((eighth * at.own_class) % parts).astype(F32) * (2.0 * np.pi / parts)
    sigma = jnp.full((parts,), 1.0, F32) * (1.0 - 2.0 * at.half.astype(F32))
    phases = jnp.stack([jnp.cos(angle), -jnp.sin(angle), sigma])
    short = np.arange(long)
    angle = (np.arange(half)[:, None] * short[None, :] % long) * (2.0 * np.pi / long)
    base_cos, base_sin = jnp.asarray(np.cos(angle), F32), jnp.asarray(-np.sin(angle), F32)
    forth, back = [], []
    for offset in offsets:
        angle = ((jnp.arange(long, dtype=jnp.int32) * offset) % G).astype(F32) * (2.0 * np.pi / G)
        c, s = jnp.cos(angle)[None, :], -jnp.sin(angle)[None, :]
        real, imag = base_cos * c - base_sin * s, base_cos * s + base_sin * c
        forth.append(jnp.concatenate([real, imag], axis=0))
        back.append(jnp.concatenate([real.T, imag.T], axis=0))
    short = np.arange(LONG)
    angle = (short[:, None] * short[None, :] % LONG) * (2.0 * np.pi / LONG)
    inner = split_table(np.concatenate([np.cos(angle), -np.sin(angle)], axis=1))
    angle = np.arange(RADIX)[:, None] * short[None, :] * (2.0 * np.pi / G)
    twist = jnp.asarray(np.concatenate([np.cos(angle), -np.sin(angle)], axis=0).astype(np.float32))

    split = radix == 2 and width % (2 * classes * 8) == 0 and classes * 2 == slabs
    out_shape = [shape_of(blocks, 4, tiles, capacity), shape_of(blocks, 2, tiles, capacity)]
    operands = [stat, targ]
    if split:
        kept = width // slabs
        pieces = pl.pallas_call(
            turn_kernel,
            out_shape=shape_of(slabs, RADIX, kept, LONG),
            scratch_shapes=[pltpu.VMEM((LONG // TC, width, TC), F32)],
            name="turn",
        )(spectrum)
        operands.append(pieces)
        out_shape.append(shape_of(slabs, RADIX, kept, LONG))
    sems = [dma(slabs), dma(blocks), dma(classes), dma(blocks), dma(slabs), dma(slabs), dma()]
    collected = talk(
        functools.partial(collect_kernel, split), out_shape, sems, 0, "collect"
    )(*operands)
    if split:
        groups = [[at.deep * i + j for i in range(ranks)] for j in range(at.deep)]
        factors = lax.all_gather(collected[2], "slab", axis_index_groups=groups, axis=0, tiled=True)
        if kept != 8:
            factors = factors.transpose(1, 0, 2, 3).reshape(RADIX, half // 8, 8, LONG)
            factors = factors.transpose(1, 0, 2, 3)
    else:
        everything = lax.all_gather(spectrum, ("slab", "rhs"), axis=1, tiled=True)
        columns = offsets[0] + classes * radix * jnp.arange(half)
        chosen = jnp.take(everything, columns, axis=1).T
        factors = chosen.reshape(half // 8, 8, LONG, RADIX).transpose(0, 3, 1, 2)

    main, rim = shape_of(blocks, 2, half, rows), shape_of(2, half, TC)
    folds = fold // TC
    field = pltpu.VMEM((blocks, 2, folds, TC, rows), F32)
    vmem, smem = pl.BlockSpec(memory_space=pltpu.VMEM), pl.BlockSpec(memory_space=pltpu.SMEM)

    def swap(main_value, rim_value):
        return talk(pair_kernel, [main, rim], [dma(2), dma(2)], 1, "pair")(main_value, rim_value)

    def smoothed(direction):
        own, own_rim, oth, oth_rim = pl.pallas_call(
            spread_kernel,
            out_shape=[main, rim, main, rim],
            in_specs=[vmem, vmem, smem, vmem, vmem],
            scratch_shapes=[field, pltpu.VMEM((blocks, 2, folds, TC, RIM), F32)],
            name="spread",
        )(collected[0], direction, phases, *forth)
        got, got_rim = swap(oth, oth_rim)
        keep, keep_rim, give, give_rim = pl.pallas_call(
            middle_kernel,
            out_shape=[main, rim, main, rim],
            scratch_shapes=[pltpu.VMEM((RADIX, 2, half, LONG), F32)],
            name="middle",
        )(own, own_rim, got, got_rim, factors, *inner, twist)
        got, got_rim = swap(give, give_rim)
        return pl.pallas_call(
            gather_kernel,
            out_shape=shape_of(*direction.shape),
            in_specs=[vmem, smem] + [vmem] * 6,
            scratch_shapes=[field, pltpu.VMEM((blocks + 1, 2, folds, TC, RIM), F32)],
            name="gather",
        )(collected[0], phases, *back, keep, keep_rim, got, got_rim)

    residual = collected[1]
    solution = jnp.zeros(residual.shape, F32)
    direction = residual
    points = shape_of(*residual.shape)
    for repeat in range(ITERS):
        last = repeat + 1 == ITERS
        direction, residual, solution = talk(
            functools.partial(update_kernel, last),
            [points] * 3,
            [
                pltpu.VMEM((classes, *residual.shape), F32),
                pltpu.VMEM((2, 8, TC), F32),
                pltpu.VMEM((2, 8, TC), F32),
                dma(classes),
                dma(classes),
                dma(2),
                dma(2),
            ],
            2 + last,
            "update",
            pltpu.VMEM,
            (4,),
        )(smoothed(direction), direction, residual, solution, noise_var)
    out = shape_of(2, tiles, capacity)
    solution, residual = talk(deliver_kernel, [out, out], [dma(2), dma(2)], 4, "deliver")(
        solution, residual
    )
    return (solution, residual)


def solution(mesh):
    placed = (
        P("rhs", "slab", None),
        P("slab"),
        P("slab", None),
        P("slab", None),
        P(None, "slab", None),
        P(None, ("slab", "rhs")),
        P(),
    )
    return jax.shard_map(
        per_device,
        mesh=mesh,
        in_specs=placed,
        out_specs=(P("rhs", "slab", None), P("rhs", "slab", None)),
        check_vma=False,
    )
```

time: 566 us -> 302 us (0.53)
  Pallas kernels: 510 us -> 274 us
  blocking collectives: 19.1 us -> 0 us
    pallas_call x14 -> x15, Pallas kernels: 510 us -> 274 us  [the longest x2 86.5 us: smoothed(): pl.pallas_call(spread_kernel, out_shape=[main, rim, main, rim], in_specs=...]
    all_to_all x1 -> x0, blocking collectives: 19.1 us -> none  [exchanged_spectrum(): lax.all_to_all(turned.reshape(count, kept, G), 'slab', 0, 0, tiled=True)]
  transfers between devices with their start and end apart: 1 -> 1, of which waited for: 0 -> 0; matrix products, arithmetic and copies ran while one was open for 0% -> 2% of each run, Pallas kernels for 16% -> 16%
where the time goes in v1:
time: 302 us; the launch traced here: 301 us
  Pallas kernels  274 us (91%)
  between operations  14.9 us (5%)
  local copies, waits for them, and re-layouts  7.97 us (3%)
  other arithmetic  4.88 us (2%)
    pallas_call x2, Pallas kernels, smoothed(): pl.pallas_call(spread_kernel, out_shape=[main, rim, main, rim], in_specs=...  86.5 us
    pallas_call x2, Pallas kernels, smoothed(): pl.pallas_call(gather_kernel, out_shape=shape_of(*direction.shape), in_sp...  76.8 us
    pallas_call x8, Pallas kernels, call(): pl.pallas_call(kernel, out_shape=out_shape, in_specs=specs, out_specs=[pl...  70.5 us
    pallas_call x2, Pallas kernels, smoothed(): pl.pallas_call(middle_kernel, out_shape=[main, rim, main, rim], scratch_s...  37.5 us
  transfers between devices with their start and end apart: 1, of which 0 were waited for; matrix products, arithmetic and copies ran while one was open for 2% of the time, Pallas kernels for 16%

profile of v1, /device:TPU:5, one launch (start us, length us, event | category | flops | bytes accessed | tf_op | source)
XLA Modules:
  0.0 301.4 jit_solution(4653443551312341172)
XLA Ops:
  7.3 0.7 iota_compare_fusion
  8.0 2.5 copy.19.spectrum
  10.5 2.4 turn.1.refs_2_
  12.9 0.1 convert_bitcast_fusion
  12.9 0.6 broadcast_select_fusion.refs_1_
  13.6 0.6 pad_maximum_fusion.4.refs_0_
  14.2 18.2 %collect.1 = (f32[4,4,16,256]{3,2,1,0:T(8,128)}, f32[4,2,16,256]{3,2,1,0:T(8,128)}, f32[8,8,8,256]{3,2,1,0:T(8,128)}) custom-call(f32[4,16,256]{2,1,0:T(8,128)} %pad_maximum_fusion.4.refs_0_, f32[2,16,256]{2,1,0:T(8,128)} %broadcast_select_fusion.refs_1_, f32[8,8,8,256]{3,2,1,0:T(8,128)} %turn.1.refs_2_), custom_call_target="tpu_custom_call" | custom-call | tf_op jit(solution)/shard_map/collect/pallas_call | solution.py:627
  32.6 0.2 multiply_subtract_fusion
  32.8 0.1 pad_maximum_fusion.2
  32.9 1.0 copy.20.tab_own
  33.9 0.1 pad_maximum_fusion.3
  33.9 1.0 copy.21.tab_oth
  35.6 0.1 pad.10.clone
  35.7 0.7 maximum_maximum_fusion.phases
  36.4 43.2 %spread.2 = (f32[4,2,256,256]{3,2,1,0:T(8,128)}, f32[2,256,128]{2,1,0:T(8,128)}, f32[4,2,256,256]{3,2,1,0:T(8,128)}, f32[2,256,128]{2,1,0:T(8,128)}) custom-call(f32[4,4,16,256]{3,2,1,0:T(8,128)} %get-tuple-element.34.stat, f32[4,2,16,256]{3,2,1,0:T(8,128)} %get-tuple-element.35.vec.direction.residual, f32[3,8]{1,0:T(4,128)} %maximum_maximum_fusion.phases, ...), custom_call_target="tpu_custom_call" | custom-call | tf_op jit(solution)/shard_map/spread/pallas_call | solution.py:728
  79.6 4.9 %pair.4 = (f32[4,2,256,256]{3,2,1,0:T(8,128)}, f32[2,256,128]{2,1,0:T(8,128)}) custom-call(f32[4,2,256,256]{3,2,1,0:T(8,128)} %get-tuple-element.38.main, f32[2,256,128]{2,1,0:T(8,128)} %get-tuple-element.39.rim), custom_call_target="tpu_custom_call" | custom-call | tf_op jit(solution)/shard_map/pair/pallas_call | solution.py:627
  84.5 0.9 pad_maximum_fusion.tab_own
  85.4 0.8 pad_maximum_fusion.1.tab_oth
  86.2 18.8 %middle.2 = (f32[4,2,256,256]{3,2,1,0:T(8,128)}, f32[2,256,128]{2,1,0:T(8,128)}, f32[4,2,256,256]{3,2,1,0:T(8,128)}, f32[2,256,128]{2,1,0:T(8,128)}) custom-call(f32[4,2,256,256]{3,2,1,0:T(8,128)} %get-tuple-element.36.own, f32[2,256,128]{2,1,0:T(8,128)} %get-tuple-element.37.own_rim, f32[4,2,256,256]{3,2,1,0:T(8,128)} %get-tuple-element.40.got, ...), custom_call_target="tpu_custom_call" | custom-call | tf_op jit(solution)/shard_map/middle/pallas_call | solution.py:736
  105.0 4.9 %pair.5 = (f32[4,2,256,256]{3,2,1,0:T(8,128)}, f32[2,256,128]{2,1,0:T(8,128)}) custom-call(f32[4,2,256,256]{3,2,1,0:T(8,128)} %get-tuple-element.45.main, f32[2,256,128]{2,1,0:T(8,128)} %get-tuple-element.46.rim), custom_call_target="tpu_custom_call" | custom-call | tf_op jit(solution)/shard_map/pair/pallas_call | solution.py:627
  109.9 38.4 %gather.2.partial = f32[4,2,16,256]{3,2,1,0:T(8,128)} custom-call(f32[4,4,16,256]{3,2,1,0:T(8,128)} %get-tuple-element.34.stat, f32[3,8]{1,0:T(4,128)} %maximum_maximum_fusion.phases, f32[512,256]{1,0:T(8,128)} %pad_maximum_fusion.tab_own, f32[512,256]{1,0:T(8,128)} %pad_maximum_fusion.1.tab_oth, f32[4,2,256,256]{3,2,1,0:T(8,128)} %get-tuple-element.43.own, ...), custom_call_target="tpu_custom_call" | custom-call | tf_op jit(solution)/shard_map/gather/pallas_call | solution.py:743
  148.3 0.6 broadcast_in_dim.28.solution
  148.9 13.4 %update.2 = (f32[4,2,16,256]{3,2,1,0:T(8,128)}, f32[4,2,16,256]{3,2,1,0:T(8,128)}, f32[4,2,16,256]{3,2,1,0:T(8,128)}) custom-call(f32[4,2,16,256]{3,2,1,0:T(8,128)} %gather.2.partial, f32[4,2,16,256]{3,2,1,0:T(8,128)} %get-tuple-element.35.vec.direction.residual, f32[4,2,16,256]{3,2,1,0:T(8,128)} %get-tuple-element.35.vec.direction.residual, ...), custom_call_target="tpu_custom_call" | custom-call | tf_op jit(solution)/shard_map/update/pallas_call | solution.py:627
  162.3 43.3 %spread.3 = (f32[4,2,256,256]{3,2,1,0:T(8,128)}, f32[2,256,128]{2,1,0:T(8,128)}, f32[4,2,256,256]{3,2,1,0:T(8,128)}, f32[2,256,128]{2,1,0:T(8,128)}) custom-call(f32[4,4,16,256]{3,2,1,0:T(8,128)} %get-tuple-element.34.stat, f32[4,2,16,256]{3,2,1,0:T(8,128)} %get-tuple-element.49.vec.direction, f32[3,8]{1,0:T(4,128)} %maximum_maximum_fusion.phases, ...), custom_call_target="tpu_custom_call" | custom-call | tf_op jit(solution)/shard_map/spread/pallas_call | solution.py:728
  205.6 4.9 %pair.6 = (f32[4,2,256,256]{3,2,1,0:T(8,128)}, f32[2,256,128]{2,1,0:T(8,128)}) custom-call(f32[4,2,256,256]{3,2,1,0:T(8,128)} %get-tuple-element.52.main, f32[2,256,128]{2,1,0:T(8,128)} %get-tuple-element.53.rim), custom_call_target="tpu_custom_call" | custom-call | tf_op jit(solution)/shard_map/pair/pallas_call | solution.py:627
  210.5 18.7 %middle.3 = (f32[4,2,256,256]{3,2,1,0:T(8,128)}, f32[2,256,128]{2,1,0:T(8,128)}, f32[4,2,256,256]{3,2,1,0:T(8,128)}, f32[2,256,128]{2,1,0:T(8,128)}) custom-call(f32[4,2,256,256]{3,2,1,0:T(8,128)} %get-tuple-element.50.own, f32[2,256,128]{2,1,0:T(8,128)} %get-tuple-element.51.own_rim, f32[4,2,256,256]{3,2,1,0:T(8,128)} %get-tuple-element.54.got, ...), custom_call_target="tpu_custom_call" | custom-call | tf_op jit(solution)/shard_map/middle/pallas_call | solution.py:736
  229.3 4.9 %pair.7 = (f32[4,2,256,256]{3,2,1,0:T(8,128)}, f32[2,256,128]{2,1,0:T(8,128)}) custom-call(f32[4,2,256,256]{3,2,1,0:T(8,128)} %get-tuple-element.58.main, f32[2,256,128]{2,1,0:T(8,128)} %get-tuple-element.59.rim), custom_call_target="tpu_custom_call" | custom-call | tf_op jit(solution)/shard_map/pair/pallas_call | solution.py:627
  234.2 38.4 %gather.3.partial = f32[4,2,16,256]{3,2,1,0:T(8,128)} custom-call(f32[4,4,16,256]{3,2,1,0:T(8,128)} %get-tuple-element.34.stat, f32[3,8]{1,0:T(4,128)} %maximum_maximum_fusion.phases, f32[512,256]{1,0:T(8,128)} %pad_maximum_fusion.tab_own, f32[512,256]{1,0:T(8,128)} %pad_maximum_fusion.1.tab_oth, f32[4,2,256,256]{3,2,1,0:T(8,128)} %get-tuple-element.56.own, ...), custom_call_target="tpu_custom_call" | custom-call | tf_op jit(solution)/shard_map/gather/pallas_call | solution.py:743
  272.6 12.4 %update.3 = (f32[4,2,16,256]{3,2,1,0:T(8,128)}, f32[4,2,16,256]{3,2,1,0:T(8,128)}, f32[4,2,16,256]{3,2,1,0:T(8,128)}) custom-call(f32[4,2,16,256]{3,2,1,0:T(8,128)} %gather.3.partial, f32[4,2,16,256]{3,2,1,0:T(8,128)} %get-tuple-element.49.vec.direction, f32[4,2,16,256]{3,2,1,0:T(8,128)} %get-tuple-element.62.residual, ...), custom_call_target="tpu_custom_call" | custom-call | tf_op jit(solution)/shard_map/update/pallas_call | solution.py:627
  285.0 6.8 %deliver.1 = (f32[2,16,256]{2,1,0:T(8,128)}, f32[2,16,256]{2,1,0:T(8,128)}) custom-call(f32[4,2,16,256]{3,2,1,0:T(8,128)} %get-tuple-element.64.solution, f32[4,2,16,256]{3,2,1,0:T(8,128)} %get-tuple-element.65.residual), custom_call_target="tpu_custom_call" | custom-call | tf_op jit(solution)/shard_map/deliver/pallas_call | solution.py:627
  291.8 1.4 copy.27
  293.2 1.4 copy.28
  (20 shorter events, 0.2 us)
Async XLA Ops:
  7.2 5.7 %copy-start.6 = (s32[16]{0:T(128)S(1)}, s32[16]{0:T(128)}, u32[]{:S(2)}) copy-start(s32[16]{0:T(128)} %param.13) | copy-start | bytes 196
  7.2 5.7 %copy-start.4 = (s32[16,256]{1,0:T(8,128)S(1)}, s32[16,256]{1,0:T(8,128)}, u32[]{:S(2)}) copy-start(s32[16,256]{1,0:T(8,128)} %param.15) | copy-start | bytes 49156
  7.2 5.7 %copy-start.5 = (s32[16,256]{1,0:T(8,128)S(1)}, s32[16,256]{1,0:T(8,128)}, u32[]{:S(2)}) copy-start(s32[16,256]{1,0:T(8,128)} %param.14) | copy-start | bytes 49156
  7.2 5.7 %copy-start.2 = (f32[2,16,256]{2,1,0:T(8,128)S(1)}, f32[2,16,256]{2,1,0:T(8,128)}, u32[]{:S(2)}) copy-start(f32[2,16,256]{2,1,0:T(8,128)} %param.12) | copy-start | bytes 98308
  7.2 6.4 %copy-start.3 = (f32[2,16,256]{2,1,0:T(8,128)S(1)}, f32[2,16,256]{2,1,0:T(8,128)}, u32[]{:S(2)}) copy-start(f32[2,16,256]{2,1,0:T(8,128)} %param.16) | copy-start | bytes 98308
  7.2 79.0 %all-gather.2.cloned.1.call-start = ((), (), s32[]{:S(2)}) async-start(), calls=%async_computation | async-start | bytes 2621440 | tf_op jit(solution)/shard_map/all_gather | solution.py:709
  8.0 24.6 %copy-start = (f32[256,256]{0,1:T(8,128)S(1)}, f32[256,256]{0,1:T(8,128)}, u32[]{:S(2)}) copy-start(f32[256,256]{0,1:T(8,128)} %constant.79.clone) | copy-start | bytes 786436
  8.0 24.6 %copy-start.1 = (f32[256,256]{0,1:T(8,128)S(1)}, f32[256,256]{0,1:T(8,128)}, u32[]{:S(2)}) copy-start(f32[256,256]{0,1:T(8,128)} %constant.78.clone) | copy-start | bytes 786436
Sparse Core Ops, SparseCore 0:
  32.6 44.8 all-gather.1
